TPU v7x, 32 devices: a whole 2x2x4 slice. The times are simulated.
32 devices in a mesh: group: 4 (over y, x), fsdp: 2 (over core), tensor: 4 (over z).
Axes of the slice: x: 2, y: 2, z: 4, core: 2. Of those that a mesh axis runs over, the one named last changes fastest.
Arguments:
- patches: bfloat16 [4, 2, 8, 577, 1024], P('group', None, ('fsdp', 'tensor')), may hold values from -6 to 6
- output_grad: bfloat16 [4, 2, 8, 577, 1024], P('group', None, ('fsdp', 'tensor')), may hold values from -6 to 6
- live_counts: int32 [4, 2, 2], P('group'), may hold values from 1 to 4, as said below
- attn_master: float32 [4, 1024, 1024], P(None, 'fsdp', 'tensor')
- mlp_master: float32 [2, 1024, 4096], P(None, 'fsdp', 'tensor')
- vector_master: float32 [12, 1024], replicated
- attn_moments: float32 [4, 2, 4, 1024, 1024], P('group', None, None, 'fsdp', 'tensor'), as said below
- mlp_moments: float32 [4, 2, 2, 1024, 4096], P('group', None, None, 'fsdp', 'tensor'), as said below
- vector_moments: float32 [4, 2, 12, 1024], P('group'), as said below
- attn_outer: float32 [4, 1024, 1024], P(None, 'fsdp', 'tensor'), may hold values from -0.125 to 0.125
- mlp_outer: float32 [2, 1024, 4096], P(None, 'fsdp', 'tensor'), may hold values from -0.125 to 0.125
- vector_outer: float32 [12, 1024], replicated, may hold values from -0.625 to 0.625
Outputs:
- block_output: bfloat16 [4, 2, 8, 577, 1024], P('group', None, ('fsdp', 'tensor'))
- patches_grad: float32 [4, 2, 8, 577, 1024], P('group', None, ('fsdp', 'tensor'))
- attn_inner: float32 [4, 2, 4, 1024, 1024], P('group', None, None, 'fsdp', 'tensor')
- attn_state: float32 [3, 4, 1024, 1024], P(None, None, 'fsdp', 'tensor')
- attn_copy: bfloat16 [4, 1024, 1024], P(None, 'fsdp', 'tensor')
- mlp_inner: float32 [4, 2, 2, 1024, 4096], P('group', None, None, 'fsdp', 'tensor')
- mlp_state: float32 [3, 2, 1024, 4096], P(None, None, 'fsdp', 'tensor')
- mlp_copy: bfloat16 [2, 1024, 4096], P(None, 'fsdp', 'tensor')
- vector_inner: float32 [4, 2, 12, 1024], P('group')
- vector_state: float32 [3, 12, 1024], replicated
- vector_copy: bfloat16 [12, 1024], replicated
Inputs may be any that keep to these rules, and one draw needn't show every extreme that they name: live_counts[g, m, f] images are live, and they stand first, among the f-th block of 4 image slots of micro-batch m in group g; some entry equals 4. `attn_moments`: second moments are positive. `mlp_moments`: second moments are positive. `vector_moments`: second moments are positive.
All inputs are finite; a program needn't handle non-finite values.
Results may differ from a plain program's by a relative error of at most 0.012.
The roundings to bfloat16 on the way count: a program that leaves them out, or rounds other values in their place, can miss the bound.
Values may be sent and summed in bfloat16 or wider, within the bound.
A program may use at most 320 MiB of HBM per device.

v0:
```python
from functools import partial
import jax
import jax.numpy as jnp
from jax import lax
from jax.sharding import PartitionSpec as P

HD = 64
FF = 4096
STEP = 8
EPSILON = 1e-06
INNER_RATE = 0.02
VECTOR_RATE = 0.2
WEIGHT_DECAY = 0.1
OUTER_RATE = 0.7
OUTER_MOMENTUM = 0.9


def normalize(source, gain_row, shift_row):
    centre = source - jnp.mean(source, axis=-1, keepdims=True)
    spread = jnp.mean(centre * centre, axis=-1, keepdims=True)
    return centre * lax.rsqrt(spread + EPSILON) * gain_row + shift_row


def gelu_exact(source):
    return jax.nn.gelu(source, approximate=False)


def gelu_slope(source):
    return (
        0.5 * (1.0 + lax.erf(source * 0.7071067811865476))
        + source * jnp.exp(-0.5 * source * source) * 0.3989422804014327
    )


def inner_adamw(master, gradient, moments, step_rate, decay_rate):
    first_moment = 0.9 * moments[0] + 0.1 * gradient
    second_moment = 0.95 * moments[1] + 0.05 * gradient * gradient
    step_ratio = (
        first_moment / (1.0 - 0.9**STEP) / (jnp.sqrt(second_moment / (1.0 - 0.95**STEP)) + 1e-08)
    )
    return (master - step_rate * (step_ratio + decay_rate * master), second_moment)


def outer_nesterov(master, outer_old, difference):
    momentum = OUTER_MOMENTUM * outer_old + difference
    updated = master - OUTER_RATE * (difference + OUTER_MOMENTUM * momentum)
    return (jnp.stack([difference, momentum, updated]), updated.astype(jnp.bfloat16))


def attend_forward(score_scale, operands):
    queries_low, keys_low, values_low = operands
    scores = (
        jnp.einsum("qhe,khe->hqk", queries_low, keys_low, preferred_element_type=jnp.float32)
        * score_scale
    )
    highest = jnp.max(scores, axis=-1, keepdims=True)
    exponent = jnp.exp(scores - highest)
    totals = jnp.sum(exponent, axis=-1, keepdims=True)
    probs_low = (exponent / totals).astype(jnp.bfloat16)
    attended = jnp.einsum("hqk,khe->qhe", probs_low, values_low, preferred_element_type=jnp.float32)
    return (attended.astype(jnp.bfloat16), (highest + jnp.log(totals))[..., 0])


def attend_backward(score_scale, operands):
    queries_low, keys_low, values_low, log_totals, grad_attended = operands
    scores = (
        jnp.einsum("qhe,khe->hqk", queries_low, keys_low, preferred_element_type=jnp.float32)
        * score_scale
    )
    probs_full = jnp.exp(scores - log_totals[..., None])
    grad_probs = jnp.einsum(
        "qhe,khe->hqk", grad_attended, values_low, preferred_element_type=jnp.float32
    )
    grad_values = jnp.einsum(
        "hqk,qhe->khe",
        probs_full.astype(jnp.bfloat16),
        grad_attended,
        preferred_element_type=jnp.float32,
    )
    weighted = jnp.sum(probs_full * grad_probs, axis=-1, keepdims=True)
    grad_scores = (probs_full * (grad_probs - weighted)).astype(jnp.bfloat16)
    grad_queries = (
        jnp.einsum("hqk,khe->qhe", grad_scores, keys_low, preferred_element_type=jnp.float32)
        * score_scale
    )
    grad_keys = (
        jnp.einsum("hqk,qhe->khe", grad_scores, queries_low, preferred_element_type=jnp.float32)
        * score_scale
    )
    return (
        grad_queries.astype(jnp.bfloat16),
        grad_keys.astype(jnp.bfloat16),
        grad_values.astype(jnp.bfloat16),
    )


def local(
    patches,
    output_grad,
    live_counts,
    attn_master,
    mlp_master,
    vector_master,
    attn_moments,
    mlp_moments,
    vector_moments,
    attn_outer,
    mlp_outer,
    vector_outer,
):
    narrow = jnp.bfloat16
    single = jnp.float32
    tensor_index = lax.axis_index("tensor")
    fsdp_index = lax.axis_index("fsdp")
    micro_count = patches.shape[1]
    local_images = patches.shape[2]
    seq_len = patches.shape[3]
    width = patches.shape[4]
    head_cols = attn_master.shape[2]
    hidden_cols = mlp_master.shape[2]
    score_scale = HD ** (-0.5)
    attn_all, mlp_all = (
        lax.all_gather(attn_master.astype(narrow), "fsdp", axis=1, tiled=True),
        lax.all_gather(mlp_master.astype(narrow), "fsdp", axis=1, tiled=True),
    )
    bias_query = lax.dynamic_slice_in_dim(vector_master[4], tensor_index * head_cols, head_cols)
    bias_value = lax.dynamic_slice_in_dim(vector_master[5], tensor_index * head_cols, head_cols)
    head_width = attn_all.shape[2]
    heads_here = head_width // HD
    bias_hidden = lax.dynamic_slice_in_dim(
        vector_master[8:].reshape(-1), tensor_index * hidden_cols, hidden_cols
    )
    owner_counts = jnp.sum(
        jnp.where(jnp.arange(live_counts.shape[2]) == fsdp_index, live_counts[0], 0), axis=-1
    )
    slot_index = tensor_index * local_images + jnp.arange(local_images)
    alive_all = (slot_index[None, :] < owner_counts[:, None]).astype(single)
    forward_attend = partial(attend_forward, score_scale)
    backward_attend = partial(attend_backward, score_scale)
    qkv_acc = jnp.zeros((3, width, head_width), single)
    out_acc = jnp.zeros((width, head_width), single)
    fc_in_acc = jnp.zeros((width, hidden_cols), single)
    fc_out_acc = jnp.zeros((width, hidden_cols), single)
    hidden_bias_acc = jnp.zeros((hidden_cols,), single)
    query_bias_acc = jnp.zeros((head_width,), single)
    value_bias_acc = jnp.zeros((head_width,), single)
    vector_acc = jnp.zeros((6, width), single)
    outputs_mixed = []
    outputs_grad = []
    for batch_index in range(micro_count):
        inputs = patches[0, batch_index].astype(single)
        alive = alive_all[batch_index][:, None, None]
        normed_one = normalize(inputs, vector_master[0], vector_master[1]).astype(narrow)
        rows_attn = lax.all_gather(normed_one, "tensor", axis=0, tiled=True)
        image_count = rows_attn.shape[0]
        shape_heads = (image_count, seq_len, heads_here, HD)
        projected = jnp.einsum(
            "isd,jde->jise", rows_attn, attn_all[:3], preferred_element_type=single
        )
        queries_low = (projected[0] + bias_query).astype(narrow).reshape(shape_heads)
        keys_low = projected[1].astype(narrow).reshape(shape_heads)
        values_low = (projected[2] + bias_value).astype(narrow).reshape(shape_heads)
        attended, log_totals = lax.map(forward_attend, (queries_low, keys_low, values_low))
        attended = attended.reshape(image_count, seq_len, head_width)
        branch_one = lax.psum_scatter(
            jnp.einsum("ise,de->isd", attended, attn_all[3], preferred_element_type=single),
            "tensor",
            scatter_dimension=0,
            tiled=True,
        )
        resid_one = inputs + branch_one + vector_master[6]
        normed_two = normalize(resid_one, vector_master[2], vector_master[3]).astype(narrow)
        rows_mlp = lax.all_gather(normed_two, "tensor", axis=0, tiled=True)
        pre_act = (
            jnp.einsum("isd,df->isf", rows_mlp, mlp_all[0], preferred_element_type=single)
            + bias_hidden
        )
        hidden = gelu_exact(pre_act).astype(narrow)
        branch_two = lax.psum_scatter(
            jnp.einsum("isf,df->isd", hidden, mlp_all[1], preferred_element_type=single),
            "tensor",
            scatter_dimension=0,
            tiled=True,
        )
        outputs_mixed.append((alive * (resid_one + branch_two + vector_master[7])).astype(narrow))
        grad_out = alive * output_grad[0, batch_index].astype(single)
        rows_grad_two = lax.all_gather(grad_out.astype(narrow), "tensor", axis=0, tiled=True)
        fc_out_acc = fc_out_acc + jnp.einsum(
            "isd,isf->df", rows_grad_two, hidden, preferred_element_type=single
        )
        grad_hidden = jnp.einsum(
            "isd,df->isf", rows_grad_two, mlp_all[1], preferred_element_type=single
        )
        grad_pre = (grad_hidden * gelu_slope(pre_act)).astype(narrow)
        fc_in_acc = fc_in_acc + jnp.einsum(
            "isd,isf->df", rows_mlp, grad_pre, preferred_element_type=single
        )
        hidden_bias_acc = hidden_bias_acc + jnp.sum(grad_pre.astype(single), axis=(0, 1))
        grad_normed_two = lax.psum_scatter(
            jnp.einsum("isf,df->isd", grad_pre, mlp_all[0], preferred_element_type=single),
            "tensor",
            scatter_dimension=0,
            tiled=True,
        )
        unused_two, norm_pull_two = jax.vjp(
            normalize, resid_one, vector_master[2], vector_master[3]
        )
        back_resid, gain_two, shift_two = norm_pull_two(grad_normed_two)
        grad_resid = grad_out + back_resid
        rows_grad_one = lax.all_gather(grad_resid.astype(narrow), "tensor", axis=0, tiled=True)
        out_acc = out_acc + jnp.einsum(
            "isd,ise->de", rows_grad_one, attended, preferred_element_type=single
        )
        grad_attended = jnp.einsum(
            "isd,de->ise", rows_grad_one, attn_all[3], preferred_element_type=single
        ).astype(narrow)
        grad_queries, grad_keys, grad_values = lax.map(
            backward_attend,
            (queries_low, keys_low, values_low, log_totals, grad_attended.reshape(shape_heads)),
        )
        grad_queries = grad_queries.reshape(image_count, seq_len, head_width)
        grad_keys = grad_keys.reshape(image_count, seq_len, head_width)
        grad_values = grad_values.reshape(image_count, seq_len, head_width)
        grad_stack = jnp.stack([grad_queries, grad_keys, grad_values])
        qkv_acc = qkv_acc + jnp.einsum(
            "isd,jise->jde", rows_attn, grad_stack, preferred_element_type=single
        )
        query_bias_acc = query_bias_acc + jnp.sum(grad_queries.astype(single), axis=(0, 1))
        value_bias_acc = value_bias_acc + jnp.sum(grad_values.astype(single), axis=(0, 1))
        summed = jnp.einsum("ise,de->isd", grad_queries, attn_all[0], preferred_element_type=single)
        summed = summed + jnp.einsum(
            "ise,de->isd", grad_keys, attn_all[1], preferred_element_type=single
        )
        grad_normed_one = lax.psum_scatter(
            summed
            + jnp.einsum("ise,de->isd", grad_values, attn_all[2], preferred_element_type=single),
            "tensor",
            scatter_dimension=0,
            tiled=True,
        )
        unused_one, norm_pull_one = jax.vjp(normalize, inputs, vector_master[0], vector_master[1])
        back_inputs, gain_one, shift_one = norm_pull_one(grad_normed_one)
        outputs_grad.append(grad_resid + back_inputs)
        vector_acc = vector_acc + jnp.stack(
            [
                gain_one,
                shift_one,
                gain_two,
                shift_two,
                jnp.sum(grad_resid, axis=(0, 1)),
                jnp.sum(grad_out, axis=(0, 1)),
            ]
        )
    attn_grad_full = jnp.concatenate([qkv_acc, out_acc[None]], 0)
    query_row = lax.dynamic_update_slice_in_dim(
        jnp.zeros((width,), single), query_bias_acc, tensor_index * head_cols, 0
    )
    value_row = lax.dynamic_update_slice_in_dim(
        jnp.zeros((width,), single), value_bias_acc, tensor_index * head_cols, 0
    )
    mlp_grad_cols = jnp.stack([fc_in_acc, fc_out_acc])
    attn_grad, mlp_grad = (
        lax.psum_scatter(attn_grad_full, "fsdp", scatter_dimension=1, tiled=True),
        lax.psum_scatter(mlp_grad_cols, "fsdp", scatter_dimension=1, tiled=True),
    )
    hidden_rows = lax.dynamic_update_slice_in_dim(
        jnp.zeros((FF,), single), hidden_bias_acc, tensor_index * hidden_cols, 0
    ).reshape(-1, width)
    vector_part = jnp.concatenate(
        [vector_acc[:4], jnp.stack([query_row, value_row]), vector_acc[4:], hidden_rows], 0
    )
    vector_grad = lax.psum(vector_part, ("fsdp", "tensor"))
    new_attn, second_attn = inner_adamw(
        attn_master, attn_grad, attn_moments[0], INNER_RATE, WEIGHT_DECAY
    )
    new_mlp, second_mlp = inner_adamw(
        mlp_master, mlp_grad, mlp_moments[0], INNER_RATE, WEIGHT_DECAY
    )
    new_vector, second_vector = inner_adamw(
        vector_master, vector_grad, vector_moments[0], VECTOR_RATE, 0.0
    )
    diff_attn, diff_mlp, diff_vector = lax.psum(
        (attn_master - new_attn, mlp_master - new_mlp, vector_master - new_vector), "group"
    )
    groups = lax.axis_size("group")
    attn_state, attn_copy = outer_nesterov(attn_master, attn_outer, diff_attn / groups)
    mlp_state, mlp_copy = outer_nesterov(mlp_master, mlp_outer, diff_mlp / groups)
    vector_state, vector_copy = outer_nesterov(vector_master, vector_outer, diff_vector / groups)
    block_output = jnp.stack(outputs_mixed)[None]
    patches_grad = jnp.stack(outputs_grad)[None]
    attn_inner = jnp.stack([attn_grad, second_attn])[None]
    mlp_inner = jnp.stack([mlp_grad, second_mlp])[None]
    vector_inner = jnp.stack([vector_grad, second_vector])[None]
    return (
        block_output,
        patches_grad,
        attn_inner,
        attn_state,
        attn_copy,
        mlp_inner,
        mlp_state,
        mlp_copy,
        vector_inner,
        vector_state,
        vector_copy,
    )


def solution(mesh):
    placed = (
        P("group", None, ("fsdp", "tensor"), None, None),
        P("group", None, ("fsdp", "tensor"), None, None),
        P("group", None, None),
        P(None, "fsdp", "tensor"),
        P(None, "fsdp", "tensor"),
        P(),
        P("group", None, None, "fsdp", "tensor"),
        P("group", None, None, "fsdp", "tensor"),
        P("group", None, None, None),
        P(None, "fsdp", "tensor"),
        P(None, "fsdp", "tensor"),
        P(),
    )
    return jax.shard_map(
        local,
        mesh=mesh,
        in_specs=placed,
        out_specs=(
            P("group", None, ("fsdp", "tensor"), None, None),
            P("group", None, ("fsdp", "tensor"), None, None),
            P("group", None, None, "fsdp", "tensor"),
            P(None, None, "fsdp", "tensor"),
            P(None, "fsdp", "tensor"),
            P("group", None, None, "fsdp", "tensor"),
            P(None, None, "fsdp", "tensor"),
            P(None, "fsdp", "tensor"),
            P("group", None, None, None),
            P(),
            P(),
        ),
        check_vma=False,
    )
```

profile of v0, /device:TPU:0, one launch (start us, length us, event | category | flops | bytes accessed | tf_op | source)
XLA Modules:
  0.0 2521.2 jit_solution(1555532051777853854)
XLA Ops:
  23.5 93.8 %all-gather.19.cloned.1.call-done = bf16[4,577,1024]{2,1,0:T(8,128)(2,1)} async-done(((bf16[1,577,1024]{2,1,0:T(8,128)(2,1)}), bf16[4,577,1024]{2,1,0:T(8,128)(2,1)}) %all-gather.19.cloned.1.call-update) | async-done | bytes 4726800 | tf_op jit(solution)/shard_map/all_gather | solution.py:154
  126.6 81.9 %all-gather.11.cloned.1.call-done = bf16[4,577,1024]{2,1,0:T(8,128)(2,1)} async-done(((bf16[1,577,1024]{2,1,0:T(8,128)(2,1)}), bf16[4,577,1024]{2,1,0:T(8,128)(2,1)}) %all-gather.11.cloned.1.call-update) | async-done | bytes 4726800 | tf_op jit(solution)/shard_map/all_gather | solution.py:154
  240.4 25.3 %while.53 = (s32[]{:T(128)}, bf16[4,577,4,64]{1,3,2,0:T(8,128)(2,1)}, f32[4,4,577]{2,1,0:T(4,128)S(1)}, bf16[4,577,4,64]{1,3,2,0:T(8,128)(2,1)}, bf16[4,577,4,64...) while((s32[]{:T(128)}, bf16[4,577,4,64]{1,3,2,0:T(8,128)(2,1)}, ...), condition=%wide.region_16.17_spmd, body=%wide.region_13.16_spmd.sunk | while | flops 353050112 | bytes 17370320 | solution.py:163
  279.1 21.4 while.52
  312.4 122.7 %reduce-scatter.15.cloned.1.call-done = f32[1,577,1024]{2,1,0:T(8,128)} async-done(((f32[4,577,1024]{2,1,0:T(8,128)}), f32[1,577,1024]{2,1,0:T(8,128)}) %reduce-scatter.15.cloned.1.call-update) | async-done | bytes 2363408 | tf_op jit(solution)/shard_map/reduce_scatter | solution.py:165
  435.1 167.2 %reduce-scatter.11.cloned.1.call-done = f32[1,577,1024]{2,1,0:T(8,128)} async-done(((f32[4,577,1024]{2,1,0:T(8,128)}), f32[1,577,1024]{2,1,0:T(8,128)}) %reduce-scatter.11.cloned.1.call-update) | async-done | bytes 2363408 | tf_op jit(solution)/shard_map/reduce_scatter | solution.py:165
  629.3 83.4 %all-gather.21.cloned.1.call-done = bf16[4,577,1024]{2,1,0:T(8,128)(2,1)} async-done(((bf16[1,577,1024]{2,1,0:T(8,128)(2,1)}), bf16[4,577,1024]{2,1,0:T(8,128)(2,1)}) %all-gather.21.cloned.1.call-update) | async-done | bytes 4726800 | tf_op jit(solution)/shard_map/all_gather | solution.py:173
  712.7 10.2 fusion.225
  722.9 80.9 %all-gather.15.cloned.1.call-done = bf16[4,577,1024]{2,1,0:T(8,128)(2,1)} async-done(((bf16[1,577,1024]{2,1,0:T(8,128)(2,1)}), bf16[4,577,1024]{2,1,0:T(8,128)(2,1)}) %all-gather.15.cloned.1.call-update) | async-done | bytes 4726800 | tf_op jit(solution)/shard_map/all_gather | solution.py:173
  803.8 20.2 fusion.210
  824.0 70.3 %all-gather.23.cloned.1.call-done = bf16[4,577,1024]{2,1,0:T(8,128)(2,1)} async-done(((bf16[1,577,1024]{2,1,0:T(8,128)(2,1)}), bf16[4,577,1024]{2,1,0:T(8,128)(2,1)}) %all-gather.23.cloned.1.call-update) | async-done | bytes 4726800 | tf_op jit(solution)/shard_map/all_gather | solution.py:187
  894.3 12.3 convert_reduce_fusion.1
  917.0 67.8 %all-gather.27.cloned.1.call-done = bf16[4,577,1024]{2,1,0:T(8,128)(2,1)} async-done(((bf16[1,577,1024]{2,1,0:T(8,128)(2,1)}), bf16[4,577,1024]{2,1,0:T(8,128)(2,1)}) %all-gather.27.cloned.1.call-update) | async-done | bytes 4726800 | tf_op jit(solution)/shard_map/all_gather | solution.py:187
  984.7 12.5 convert_reduce_fusion
  1007.1 46.6 %fusion.116 = (bf16[4,577,1024]{2,1,0:T(8,128)(2,1)S(1)}, bf16[4,577,1024]{2,1,0:T(8,128)(2,1)}) fusion(f32[4,577,1024]{2,1,0:T(8,128)} %get-tuple-element.421, f32[1024]{0:T(1024)S(1)} %dynamic_slice.61, u8[577,1024]{1,0:T(8,128)(4,1)} %get-tuple-element.249, u8[577,1024]{1,0:T(8,128)(4,1)S(1)} %get-tuple-element.248, ...), kind=kLoop, calls=%fused_computation.127 | loop fusion | flops 333238272 | bytes 30728192 | tf_op jit(solution)/shard_map/convert_element_type | solution.py:178
  1063.8 10.6 fusion.227
  1074.5 74.4 %reduce-scatter.19.cloned.1.call-done = f32[1,577,1024]{2,1,0:T(8,128)} async-done(((f32[4,577,1024]{2,1,0:T(8,128)}), f32[1,577,1024]{2,1,0:T(8,128)}) %reduce-scatter.19.cloned.1.call-update) | async-done | bytes 2363408 | tf_op jit(solution)/shard_map/reduce_scatter | solution.py:199
  1148.9 166.6 %reduce-scatter.23.cloned.1.call-done = f32[1,577,1024]{2,1,0:T(8,128)} async-done(((f32[4,577,1024]{2,1,0:T(8,128)}), f32[1,577,1024]{2,1,0:T(8,128)}) %reduce-scatter.23.cloned.1.call-update) | async-done | bytes 2363408 | tf_op jit(solution)/shard_map/reduce_scatter | solution.py:199
  1320.8 161.4 %reduce-scatter.13.cloned.1.call-done = f32[1,577,1024]{2,1,0:T(8,128)} async-done(((f32[4,577,1024]{2,1,0:T(8,128)}), f32[1,577,1024]{2,1,0:T(8,128)}) %reduce-scatter.13.cloned.1.call-update) | async-done | bytes 2363408 | tf_op jit(solution)/shard_map/reduce_scatter | solution.py:179
  1482.1 167.2 %reduce-scatter.17.cloned.1.call-done = f32[1,577,1024]{2,1,0:T(8,128)} async-done(((f32[4,577,1024]{2,1,0:T(8,128)}), f32[1,577,1024]{2,1,0:T(8,128)}) %reduce-scatter.17.cloned.1.call-update) | async-done | bytes 2363408 | tf_op jit(solution)/shard_map/reduce_scatter | solution.py:179
  1700.8 51.3 %all-gather.29.cloned.1.call-done = bf16[4,577,1024]{2,1,0:T(8,128)(2,1)} async-done(((bf16[1,577,1024]{2,1,0:T(8,128)(2,1)}), bf16[4,577,1024]{2,1,0:T(8,128)(2,1)}) %all-gather.29.cloned.1.call-update) | async-done | bytes 4726800 | tf_op jit(solution)/shard_map/all_gather | solution.py:210
  1760.1 48.8 %while.55 = (s32[]{:T(128)}, bf16[4,577,4,64]{1,3,2,0:T(8,128)(2,1)S(1)}, bf16[4,577,4,64]{1,3,2,0:T(8,128)(2,1)}, bf16[4,577,4,64]{1,3,2,0:T(8,128)(2,1)}, bf16...) while((s32[]{:T(128)}, ...), condition=%wide.region_35.36_spmd, body=%wide.region_33.35_spmd.sunk | while | flops 869015040 | bytes 49660196 | solution.py:217
  1808.9 34.2 %all-gather.25.cloned.1.call-done = bf16[4,577,1024]{2,1,0:T(8,128)(2,1)} async-done(((bf16[1,577,1024]{2,1,0:T(8,128)(2,1)}), bf16[4,577,1024]{2,1,0:T(8,128)(2,1)}) %all-gather.25.cloned.1.call-update) | async-done | bytes 4726800 | tf_op jit(solution)/shard_map/all_gather | solution.py:210
  1858.7 53.2 %while.54 = (s32[]{:T(128)}, bf16[4,577,4,64]{1,3,2,0:T(8,128)(2,1)S(1)}, bf16[4,577,4,64]{1,3,2,0:T(8,128)(2,1)}, bf16[4,577,4,64]{1,3,2,0:T(8,128)(2,1)}, bf16...) while((s32[]{:T(128)}, ...), condition=%wide.region_26.27_spmd, body=%wide.region_24.26_spmd.sunk | while | flops 869015040 | bytes 49660196 | solution.py:217
  1952.0 9.5 fusion.183
  2025.6 79.9 %all-reduce.3.cloned.1.call-done = (f32[4,512,256]{1,2,0:T(8,128)}, f32[2,512,1024]{2,1,0:T(8,128)}) async-done(((f32[4,512,256]{1,2,0:T(8,128)}, f32[2,512,1024]{2,1,0:T(8,128)}), (f32[4,512,256]{1,2,0:T(8,128)}, f32[2,512,1024]{2,1,0:T(8,128)})) %all-reduce.3.cloned.1.call-update) | async-done | bytes 6291472 | tf_op jit(solution)/shard_map/psum | solution.py:282
  2120.4 13.2 fusion.262
  2133.6 12.4 pad_maximum_fusion
  2146.0 125.0 %reduce-scatter.21.cloned.1.call-done = f32[1,577,1024]{2,1,0:T(8,128)} async-done(((f32[4,577,1024]{2,1,0:T(8,128)}), f32[1,577,1024]{2,1,0:T(8,128)}) %reduce-scatter.21.cloned.1.call-update) | async-done | bytes 2363408 | tf_op jit(solution)/shard_map/reduce_scatter | solution.py:234
  2273.4 164.4 %reduce-scatter.25.cloned.1.call-done = f32[1,577,1024]{2,1,0:T(8,128)} async-done(((f32[4,577,1024]{2,1,0:T(8,128)}), f32[1,577,1024]{2,1,0:T(8,128)}) %reduce-scatter.25.cloned.1.call-update) | async-done | bytes 2363408 | tf_op jit(solution)/shard_map/reduce_scatter | solution.py:234
  2448.6 29.2 %psum.30 = f32[12,1024]{1,0:T(8,128)S(1)} all-reduce(f32[12,1024]{1,0:T(8,128)S(1)} %concatenate.7), channel_id=1, replica_groups=mesh['group'=4,'fsdp'=2,'tensor'=4] {'fsdp','tensor'}, use_global_device_ids=true, to_apply=%region_61.62 | all-reduce | flops 12288 | bytes 98304 | tf_op jit(solution)/shard_map/psum | solution.py:272
  2477.9 17.6 psum.31
  (482 shorter events, 518.1 us)
Async XLA Ops:
  7.2 16.3 all-gather.13.cloned.1.call-start
  10.1 107.3 %all-gather.19.cloned.1.call-start = ((), (), s32[]{:S(2)}) async-start(), calls=%async_computation.16 | async-start | bytes 5980160 | tf_op jit(solution)/shard_map/all_gather | solution.py:154
  19.3 189.2 %all-gather.11.cloned.1.call-start = ((), (), s32[]{:S(2)}) async-start(), calls=%async_computation.10 | async-start | bytes 5980160 | tf_op jit(solution)/shard_map/all_gather | solution.py:154
  20.0 415.1 %reduce-scatter.15.cloned.1.call-start = ((), (), s32[]{:S(2)}) async-start(), calls=%async_computation.17 | async-start | bytes 11960320 | tf_op jit(solution)/shard_map/reduce_scatter | solution.py:165
  273.1 329.1 %reduce-scatter.11.cloned.1.call-start = ((), (), s32[]{:S(2)}) async-start(), calls=%async_computation.12 | async-start | bytes 11960320 | tf_op jit(solution)/shard_map/reduce_scatter | solution.py:165
  308.4 293.9 %copy-start.65 = (f32[1,1024]{1,0:T(1,128)S(1)}, f32[1,1024]{1,0:T(1,128)}, u32[]{:S(2)}) copy-start(f32[1,1024]{1,0:T(1,128)} %get-tuple-element.393) | copy-start | bytes 12292
  308.4 320.9 %all-gather.17.cloned.1.call-start = ((), (), s32[]{:S(2)}) async-start(), calls=%async_computation.14 | async-start | bytes 6291456 | tf_op jit(solution)/shard_map/all_gather | solution.py:124
  312.3 400.3 %all-gather.21.cloned.1.call-start = ((), (), s32[]{:S(2)}) async-start(), calls=%async_computation.18 | async-start | bytes 5980160 | tf_op jit(solution)/shard_map/all_gather | solution.py:173
  609.2 194.6 %all-gather.15.cloned.1.call-start = ((), (), s32[]{:S(2)}) async-start(), calls=%async_computation.13 | async-start | bytes 5980160 | tf_op jit(solution)/shard_map/all_gather | solution.py:173
  609.9 284.4 %all-gather.23.cloned.1.call-start = ((), (), s32[]{:S(2)}) async-start(), calls=%async_computation.20 | async-start | bytes 5980160 | tf_op jit(solution)/shard_map/all_gather | solution.py:187
  623.7 361.1 %all-gather.27.cloned.1.call-start = ((), (), s32[]{:S(2)}) async-start(), calls=%async_computation.24 | async-start | bytes 5980160 | tf_op jit(solution)/shard_map/all_gather | solution.py:187
  628.2 520.7 %reduce-scatter.19.cloned.1.call-start = ((), (), s32[]{:S(2)}) async-start(), calls=%async_computation.21 | async-start | bytes 11960320 | tf_op jit(solution)/shard_map/reduce_scatter | solution.py:199
  916.9 398.6 %reduce-scatter.23.cloned.1.call-start = ((), (), s32[]{:S(2)}) async-start(), calls=%async_computation.25 | async-start | bytes 11960320 | tf_op jit(solution)/shard_map/reduce_scatter | solution.py:199
  1007.0 475.1 %reduce-scatter.13.cloned.1.call-start = ((), (), s32[]{:S(2)}) async-start(), calls=%async_computation.15 | async-start | bytes 11960320 | tf_op jit(solution)/shard_map/reduce_scatter | solution.py:179
  1063.8 585.5 %reduce-scatter.17.cloned.1.call-start = ((), (), s32[]{:S(2)}) async-start(), calls=%async_computation.19 | async-start | bytes 11960320 | tf_op jit(solution)/shard_map/reduce_scatter | solution.py:179
  1074.4 574.9 %copy-start.63 = (f32[1,1024]{1,0:T(1,128)S(1)}, f32[1,1024]{1,0:T(1,128)}, u32[]{:S(2)}) copy-start(f32[1,1024]{1,0:T(1,128)} %get-tuple-element.390) | copy-start | bytes 12292
  1074.4 677.7 %all-gather.29.cloned.1.call-start = ((), (), s32[]{:S(2)}) async-start(), calls=%async_computation.26 | async-start | bytes 5980160 | tf_op jit(solution)/shard_map/all_gather | solution.py:210
  1660.6 182.5 %all-gather.25.cloned.1.call-start = ((), (), s32[]{:S(2)}) async-start(), calls=%async_computation.22 | async-start | bytes 5980160 | tf_op jit(solution)/shard_map/all_gather | solution.py:210
  1665.2 286.8 %reduce-scatter.29.cloned.1.call-start = ((), (), s32[]{:S(2)}) async-start(), calls=%async_computation.29 | async-start | bytes 12582912 | tf_op jit(solution)/shard_map/reduce_scatter | solution.py:264
  1700.6 261.0 %reduce-scatter.27.cloned.1.call-start = ((), (), s32[]{:S(2)}) async-start(), calls=%async_computation.28 | async-start | bytes 6291456 | tf_op jit(solution)/shard_map/reduce_scatter | solution.py:263
  1937.4 168.1 %all-reduce.3.cloned.1.call-start = ((), (), s32[]{:S(2)}) async-start(), calls=%async_computation.30 | async-start | bytes 12582912 | tf_op jit(solution)/shard_map/psum | solution.py:282
  1968.6 302.4 %reduce-scatter.21.cloned.1.call-start = ((), (), s32[]{:S(2)}) async-start(), calls=%async_computation.23 | async-start | bytes 11960320 | tf_op jit(solution)/shard_map/reduce_scatter | solution.py:234
  1981.9 456.0 %reduce-scatter.25.cloned.1.call-start = ((), (), s32[]{:S(2)}) async-start(), calls=%async_computation.27 | async-start | bytes 11960320 | tf_op jit(solution)/shard_map/reduce_scatter | solution.py:234
  2133.6 137.4 %copy-start.4 = (bf16[1,1,1,577,1024]{4,3,2,1,0:T(8,128)(2,1)S(1)}, bf16[1,1,1,577,1024]{4,3,2,1,0:T(8,128)(2,1)}, u32[]{:S(2)}) copy-start(bf16[1,1,1,577,1024]{4,3,2,1,0:T(8,128)(2,1)} %copy-done.3) | copy-start | bytes 3545092
  2133.6 137.4 %copy-start.41 = (f32[1,1024]{1,0:T(1,128)S(1)}, f32[1,1024]{1,0:T(1,128)}, u32[]{:S(2)}) copy-start(f32[1,1024]{1,0:T(1,128)} %copy-done.40) | copy-start | bytes 12292
  2133.6 137.4 %copy-start.43 = (f32[577]{0:T(1024)S(1)}, f32[577]{0:T(1024)}, u32[]{:S(2)}) copy-start(f32[577]{0:T(1024)} %copy-done.42) | copy-start | bytes 6928
  2146.0 291.8 %copy-start.2 = (bf16[1,1,1,577,1024]{4,3,2,1,0:T(8,128)(2,1)S(1)}, bf16[1,1,1,577,1024]{4,3,2,1,0:T(8,128)(2,1)}, u32[]{:S(2)}) copy-start(bf16[1,1,1,577,1024]{4,3,2,1,0:T(8,128)(2,1)} %copy-done.1) | copy-start | bytes 3545092
  2146.0 291.8 %copy-start.39 = (f32[577]{0:T(1024)S(1)}, f32[577]{0:T(1024)}, u32[]{:S(2)}) copy-start(f32[577]{0:T(1024)} %copy-done.38) | copy-start | bytes 6928
  2146.0 291.8 %copy-start.49 = (f32[577]{0:T(1024)S(1)}, f32[577]{0:T(1024)}, u32[]{:S(2)}) copy-start(f32[577]{0:T(1024)} %copy-done.48) | copy-start | bytes 6928
  2273.4 168.6 %copy-start.52 = (f32[577]{0:T(1024)S(1)}, f32[577]{0:T(1024)}, u32[]{:S(2)}) copy-start(f32[577]{0:T(1024)} %copy-done.51) | copy-start | bytes 6928
  2273.4 168.7 %copy-start.47 = (f32[577]{0:T(1024)S(1)}, f32[577]{0:T(1024)}, u32[]{:S(2)}) copy-start(f32[577]{0:T(1024)} %copy-done.46) | copy-start | bytes 6928
  2273.4 168.7 %copy-start.58 = (f32[577]{0:T(1024)S(1)}, f32[577]{0:T(1024)}, u32[]{:S(2)}) copy-start(f32[577]{0:T(1024)} %copy-done.57) | copy-start | bytes 6928
  (86 other events, 780.0 us)
Sparse Core Ops, SparseCore 0:
  10.2 13.2 all-gather.12
  25.6 91.6 all-gather.18
  119.5 88.9 all-gather.10
  273.3 161.7 reduce-scatter.14
  438.0 164.2 reduce-scatter.10
  604.3 14.5 all-gather.16
  620.9 91.6 all-gather.20
  714.8 88.9 all-gather.14
  805.4 88.9 all-gather.22
  895.7 88.9 all-gather.26
  987.1 161.7 reduce-scatter.18
  1151.2 164.2 reduce-scatter.22
  1317.9 164.2 reduce-scatter.12
  1485.0 164.2 reduce-scatter.16
  1660.7 91.3 all-gather.28
  1754.1 88.9 all-gather.24
  1845.8 15.2 reduce-scatter.28
  1937.5 10.6 reduce-scatter.26
  1968.8 136.6 all-reduce.2
  2107.6 163.3 reduce-scatter.20
  2273.5 164.2 reduce-scatter.24
where the time goes:
time: 2530 us; the launch traced here: 2520 us
  waiting for transfers between devices  1800 us (71%)
  matrix products  322 us (13%)
  other arithmetic  213 us (8%)
  local copies, waits for them, and re-layouts  124 us (5%)
  blocking collectives  46.8 us (2%)
    reduce_scatter x2, waiting for transfers between devices, local(): lax.psum_scatter(jnp.einsum('isf,df->isd', hidden, mlp_all[1], preferred_...  329 us
    reduce_scatter x2, waiting for transfers between devices, local(): lax.psum_scatter(jnp.einsum('ise,de->isd', attended, attn_all[3], preferr...  290 us
    reduce_scatter x2, waiting for transfers between devices, local(): lax.psum_scatter(summed + jnp.einsum('ise,de->isd', grad_values, attn_all...  289 us
    reduce_scatter x2, waiting for transfers between devices, local(): lax.psum_scatter(jnp.einsum('isf,df->isd', grad_pre, mlp_all[0], preferre...  241 us
    all_gather x2, waiting for transfers between devices, local(): rows_attn = lax.all_gather(normed_one, 'tensor', axis=0, tiled=True)  176 us
    all_gather x2, waiting for transfers between devices, local(): rows_mlp = lax.all_gather(normed_two, 'tensor', axis=0, tiled=True)  164 us
    all_gather x2, waiting for transfers between devices, local(): lax.all_gather(grad_out.astype(narrow), 'tensor', axis=0, tiled=True)  138 us
    all_gather x2, waiting for transfers between devices, local(): lax.all_gather(grad_resid.astype(narrow), 'tensor', axis=0, tiled=True)  85.5 us
  transfers between devices with their start and end apart: 21, of which 18 were waited for; matrix products, arithmetic and copies ran while one was open for 21% of the time, Pallas kernels for 0%

commit v1 on v0

--- a/solution.py
+++ b/solution.py
@@ -13,6 +13,16 @@
 WEIGHT_DECAY = 0.1
 OUTER_RATE = 0.7
 OUTER_MOMENTUM = 0.9
+
+
+def turned_line(array, axis, d):
+    peers = lax.axis_size(axis)
+    block, shards = (array, [array])
+    for _ in range(peers - 1):
+        block = lax.ppermute(block, axis, [(i, (i + 1) % peers) for i in range(peers)])
+        shards.insert(0, block)
+    merged = jnp.concatenate(shards, axis=d)
+    return jnp.roll(merged, (lax.axis_index(axis) + 1) * array.shape[d], axis=d)
 
 
 def normalize(source, gain_row, shift_row):
@@ -151,7 +161,7 @@
         inputs = patches[0, batch_index].astype(single)
         alive = alive_all[batch_index][:, None, None]
         normed_one = normalize(inputs, vector_master[0], vector_master[1]).astype(narrow)
-        rows_attn = lax.all_gather(normed_one, "tensor", axis=0, tiled=True)
+        rows_attn = turned_line(normed_one, "tensor", 0)
         image_count = rows_attn.shape[0]
         shape_heads = (image_count, seq_len, heads_here, HD)
         projected = jnp.einsum(

time: 2530 us -> 2500 us (0.988)
  waiting for transfers between devices: 1800 us -> 1750 us
    all_gather x2 -> x0, waiting for transfers between devices: 176 us -> none  [local(): rows_attn = lax.all_gather(normed_one, 'tensor', axis=0, tiled=True)]
    ppermute x0 -> x6, waiting for transfers between devices: none -> 129 us  [turned_line(): lax.ppermute(block, axis, [(i, (i + 1) % peers) for i in range(peers)])]
    unnamed x189 -> x199, local copies, waits for them, and re-layouts: 50.9 us -> 50.3 us
  transfers between devices with their start and end apart: 21 -> 25, of which waited for: 18 -> 21; matrix products, arithmetic and copies ran while one was open for 21% -> 22% of each run, Pallas kernels for 0% -> 0%
where the time goes in v1:
time: 2500 us
  waiting for transfers between devices  1750 us (70%)
  matrix products  320 us (13%)
  other arithmetic  232 us (9%)
  local copies, waits for them, and re-layouts  122 us (5%)
  blocking collectives  46.9 us (2%)
    reduce_scatter x2, waiting for transfers between devices, local(): lax.psum_scatter(jnp.einsum('isf,df->isd', hidden, mlp_all[1], preferred_...  329 us
    reduce_scatter x2, waiting for transfers between devices, local(): lax.psum_scatter(jnp.einsum('ise,de->isd', attended, attn_all[3], preferr...  294 us
    reduce_scatter x2, waiting for transfers between devices, local(): lax.psum_scatter(summed + jnp.einsum('ise,de->isd', grad_values, attn_all...  290 us
    reduce_scatter x2, waiting for transfers between devices, local(): lax.psum_scatter(jnp.einsum('isf,df->isd', grad_pre, mlp_all[0], preferre...  241 us
    all_gather x2, waiting for transfers between devices, local(): rows_mlp = lax.all_gather(normed_two, 'tensor', axis=0, tiled=True)  164 us
    all_gather x2, waiting for transfers between devices, local(): lax.all_gather(grad_out.astype(narrow), 'tensor', axis=0, tiled=True)  138 us
    ppermute x6, waiting for transfers between devices, turned_line(): lax.ppermute(block, axis, [(i, (i + 1) % peers) for i in range(peers)])  129 us
    all_gather x2, waiting for transfers between devices, local(): lax.all_gather(grad_resid.astype(narrow), 'tensor', axis=0, tiled=True)  85.7 us
  transfers between devices with their start and end apart: 25, of which 21 were waited for; matrix products, arithmetic and copies ran while one was open for 22% of the time, Pallas kernels for 0%

profile of v1, /device:TPU:0, one launch (start us, length us, event | category | flops | bytes accessed | tf_op | source)
XLA Modules:
  0.0 2495.5 jit_solution(10322715845299574453)
XLA Ops:
  22.4 27.6 %collective-permute-done.3 = bf16[1,577,1024]{2,1,0:T(8,128)(2,1)S(1)} collective-permute-done((bf16[1,577,1024]{2,1,0:T(8,128)(2,1)S(1)}, bf16[1,577,1024]{2,1,0:T(8,128)(2,1)S(1)}, u32[]{:S(2)}, u32[]{:S(2)}) %collective-permute-start.3) | collective-permute-done | bytes 1181728 | tf_op jit(solution)/shard_map/ppermute | solution.py:22
  50.0 25.6 %collective-permute-done = bf16[1,577,1024]{2,1,0:T(8,128)(2,1)S(1)} collective-permute-done((bf16[1,577,1024]{2,1,0:T(8,128)(2,1)S(1)}, bf16[1,577,1024]{2,1,0:T(8,128)(2,1)S(1)}, u32[]{:S(2)}, u32[]{:S(2)}) %collective-permute-start) | collective-permute-done | bytes 1181728 | tf_op jit(solution)/shard_map/ppermute | solution.py:22
  75.6 25.7 %collective-permute-done.4 = bf16[1,577,1024]{2,1,0:T(8,128)(2,1)} collective-permute-done((bf16[1,577,1024]{2,1,0:T(8,128)(2,1)S(1)}, bf16[1,577,1024]{2,1,0:T(8,128)(2,1)}, u32[]{:S(2)}, u32[]{:S(2)}) %collective-permute-start.4) | collective-permute-done | bytes 1181728 | tf_op jit(solution)/shard_map/ppermute | solution.py:22
  102.7 24.2 collective-permute-done.1
  127.2 25.4 %collective-permute-done.5 = bf16[1,577,1024]{2,1,0:T(8,128)(2,1)} collective-permute-done((bf16[1,577,1024]{2,1,0:T(8,128)(2,1)}, bf16[1,577,1024]{2,1,0:T(8,128)(2,1)}, u32[]{:S(2)}, u32[]{:S(2)}) %collective-permute-start.5) | collective-permute-done | bytes 1181728 | tf_op jit(solution)/shard_map/ppermute | solution.py:22
  214.2 21.4 while.53
  246.4 22.6 while.52
  280.0 126.4 %reduce-scatter.15.cloned.1.call-done = f32[1,577,1024]{2,1,0:T(8,128)} async-done(((f32[4,577,1024]{2,1,0:T(8,128)}), f32[1,577,1024]{2,1,0:T(8,128)}) %reduce-scatter.15.cloned.1.call-update) | async-done | bytes 2363408 | tf_op jit(solution)/shard_map/reduce_scatter | solution.py:175
  406.4 167.3 %reduce-scatter.11.cloned.1.call-done = f32[1,577,1024]{2,1,0:T(8,128)} async-done(((f32[4,577,1024]{2,1,0:T(8,128)}), f32[1,577,1024]{2,1,0:T(8,128)}) %reduce-scatter.11.cloned.1.call-update) | async-done | bytes 2363408 | tf_op jit(solution)/shard_map/reduce_scatter | solution.py:175
  600.4 83.6 %all-gather.15.cloned.1.call-done = bf16[4,577,1024]{2,1,0:T(8,128)(2,1)} async-done(((bf16[1,577,1024]{2,1,0:T(8,128)(2,1)}), bf16[4,577,1024]{2,1,0:T(8,128)(2,1)}) %all-gather.15.cloned.1.call-update) | async-done | bytes 4726800 | tf_op jit(solution)/shard_map/all_gather | solution.py:183
  694.3 80.7 %all-gather.11.cloned.1.call-done = bf16[4,577,1024]{2,1,0:T(8,128)(2,1)} async-done(((bf16[1,577,1024]{2,1,0:T(8,128)(2,1)}), bf16[4,577,1024]{2,1,0:T(8,128)(2,1)}) %all-gather.11.cloned.1.call-update) | async-done | bytes 4726800 | tf_op jit(solution)/shard_map/all_gather | solution.py:183
  775.0 20.2 fusion.224
  795.2 70.4 %all-gather.17.cloned.1.call-done = bf16[4,577,1024]{2,1,0:T(8,128)(2,1)} async-done(((bf16[1,577,1024]{2,1,0:T(8,128)(2,1)}), bf16[4,577,1024]{2,1,0:T(8,128)(2,1)}) %all-gather.17.cloned.1.call-update) | async-done | bytes 4726800 | tf_op jit(solution)/shard_map/all_gather | solution.py:197
  865.5 12.3 convert_reduce_fusion.1
  888.2 67.8 %all-gather.21.cloned.1.call-done = bf16[4,577,1024]{2,1,0:T(8,128)(2,1)} async-done(((bf16[1,577,1024]{2,1,0:T(8,128)(2,1)}), bf16[4,577,1024]{2,1,0:T(8,128)(2,1)}) %all-gather.21.cloned.1.call-update) | async-done | bytes 4726800 | tf_op jit(solution)/shard_map/all_gather | solution.py:197
  956.1 12.6 convert_reduce_fusion
  978.5 46.6 %fusion.116 = (bf16[4,577,1024]{2,1,0:T(8,128)(2,1)S(1)}, bf16[4,577,1024]{2,1,0:T(8,128)(2,1)}) fusion(f32[4,577,1024]{2,1,0:T(8,128)} %get-tuple-element.422, f32[1024]{0:T(1024)S(1)} %dynamic_slice.64, u8[577,1024]{1,0:T(8,128)(4,1)} %get-tuple-element.250, u8[577,1024]{1,0:T(8,128)(4,1)S(1)} %get-tuple-element.249, ...), kind=kLoop, calls=%fused_computation.127 | loop fusion | flops 333238272 | bytes 30728192 | tf_op jit(solution)/shard_map/convert_element_type | solution.py:188
  1045.8 74.5 %reduce-scatter.19.cloned.1.call-done = f32[1,577,1024]{2,1,0:T(8,128)} async-done(((f32[4,577,1024]{2,1,0:T(8,128)}), f32[1,577,1024]{2,1,0:T(8,128)}) %reduce-scatter.19.cloned.1.call-update) | async-done | bytes 2363408 | tf_op jit(solution)/shard_map/reduce_scatter | solution.py:209
  1120.3 166.6 %reduce-scatter.23.cloned.1.call-done = f32[1,577,1024]{2,1,0:T(8,128)} async-done(((f32[4,577,1024]{2,1,0:T(8,128)}), f32[1,577,1024]{2,1,0:T(8,128)}) %reduce-scatter.23.cloned.1.call-update) | async-done | bytes 2363408 | tf_op jit(solution)/shard_map/reduce_scatter | solution.py:209
  1292.2 161.3 %reduce-scatter.13.cloned.1.call-done = f32[1,577,1024]{2,1,0:T(8,128)} async-done(((f32[4,577,1024]{2,1,0:T(8,128)}), f32[1,577,1024]{2,1,0:T(8,128)}) %reduce-scatter.13.cloned.1.call-update) | async-done | bytes 2363408 | tf_op jit(solution)/shard_map/reduce_scatter | solution.py:189
  1453.5 167.2 %reduce-scatter.17.cloned.1.call-done = f32[1,577,1024]{2,1,0:T(8,128)} async-done(((f32[4,577,1024]{2,1,0:T(8,128)}), f32[1,577,1024]{2,1,0:T(8,128)}) %reduce-scatter.17.cloned.1.call-update) | async-done | bytes 2363408 | tf_op jit(solution)/shard_map/reduce_scatter | solution.py:189
  1672.1 51.5 %all-gather.19.cloned.1.call-done = bf16[4,577,1024]{2,1,0:T(8,128)(2,1)} async-done(((bf16[1,577,1024]{2,1,0:T(8,128)(2,1)}), bf16[4,577,1024]{2,1,0:T(8,128)(2,1)}) %all-gather.19.cloned.1.call-update) | async-done | bytes 4726800 | tf_op jit(solution)/shard_map/all_gather | solution.py:220
  1731.6 48.7 %while.54 = (s32[]{:T(128)}, bf16[4,577,4,64]{1,3,2,0:T(8,128)(2,1)S(1)}, bf16[4,577,4,64]{1,3,2,0:T(8,128)(2,1)}, bf16[4,577,4,64]{1,3,2,0:T(8,128)(2,1)}, bf16...) while((s32[]{:T(128)}, ...), condition=%wide.region_26.28_spmd, body=%wide.region_24.27_spmd.sunk | while | flops 869015040 | bytes 49660196 | solution.py:227
  1780.3 34.2 %all-gather.23.cloned.1.call-done = bf16[4,577,1024]{2,1,0:T(8,128)(2,1)} async-done(((bf16[1,577,1024]{2,1,0:T(8,128)(2,1)}), bf16[4,577,1024]{2,1,0:T(8,128)(2,1)}) %all-gather.23.cloned.1.call-update) | async-done | bytes 4726800 | tf_op jit(solution)/shard_map/all_gather | solution.py:220
  1830.2 53.2 %while.55 = (s32[]{:T(128)}, bf16[4,577,4,64]{1,3,2,0:T(8,128)(2,1)S(1)}, bf16[4,577,4,64]{1,3,2,0:T(8,128)(2,1)}, bf16[4,577,4,64]{1,3,2,0:T(8,128)(2,1)}, bf16...) while((s32[]{:T(128)}, ...), condition=%wide.region_35.37_spmd, body=%wide.region_33.36_spmd.sunk | while | flops 869015040 | bytes 49660196 | solution.py:227
  1999.9 79.8 %all-reduce.3.cloned.1.call-done = (f32[4,512,256]{1,2,0:T(8,128)}, f32[2,512,1024]{2,1,0:T(8,128)}) async-done(((f32[4,512,256]{1,2,0:T(8,128)}, f32[2,512,1024]{2,1,0:T(8,128)}), (f32[4,512,256]{1,2,0:T(8,128)}, f32[2,512,1024]{2,1,0:T(8,128)})) %all-reduce.3.cloned.1.call-update) | async-done | bytes 6291472 | tf_op jit(solution)/shard_map/psum | solution.py:292
  2094.5 13.2 fusion.278
  2107.7 12.4 pad_maximum_fusion
  2120.1 125.2 %reduce-scatter.21.cloned.1.call-done = f32[1,577,1024]{2,1,0:T(8,128)} async-done(((f32[4,577,1024]{2,1,0:T(8,128)}), f32[1,577,1024]{2,1,0:T(8,128)}) %reduce-scatter.21.cloned.1.call-update) | async-done | bytes 2363408 | tf_op jit(solution)/shard_map/reduce_scatter | solution.py:244
  2247.6 164.4 %reduce-scatter.25.cloned.1.call-done = f32[1,577,1024]{2,1,0:T(8,128)} async-done(((f32[4,577,1024]{2,1,0:T(8,128)}), f32[1,577,1024]{2,1,0:T(8,128)}) %reduce-scatter.25.cloned.1.call-update) | async-done | bytes 2363408 | tf_op jit(solution)/shard_map/reduce_scatter | solution.py:244
  2422.9 29.2 %psum.30 = f32[12,1024]{1,0:T(8,128)S(1)} all-reduce(f32[12,1024]{1,0:T(8,128)S(1)} %concatenate.18), channel_id=1, replica_groups=mesh['group'=4,'fsdp'=2,'tensor'=4] {'fsdp','tensor'}, use_global_device_ids=true, to_apply=%region_61.63 | all-reduce | flops 12288 | bytes 98304 | tf_op jit(solution)/shard_map/psum | solution.py:282
  2452.2 17.7 psum.31
  (499 shorter events, 565.2 us)
Async XLA Ops:
  7.2 156.8 %all-gather.9.cloned.1.call-start = ((), (), s32[]{:S(2)}) async-start(), calls=%async_computation.10 | async-start | bytes 3145728 | tf_op jit(solution)/shard_map/all_gather | solution.py:133
  17.7 32.2 %collective-permute-start.3 = (bf16[1,577,1024]{2,1,0:T(8,128)(2,1)S(1)}, bf16[1,577,1024]{2,1,0:T(8,128)(2,1)S(1)}, u32[]{:S(2)}, u32[]{:S(2)}) collective-permute-start(bf16[1,577,1024]{2,1,0:T(8,128)(2,1)S(1)} %get-tuple-element.405), channel_id=1, source_target_pairs={{0,1},{1,2},{2,3},{3,0},{4,5},{5,6},{6,7},{7,4},{8,9},{9,10},{10,1... | collective-permute-start | bytes 3545096 | tf_op jit(solution)/shard_map/ppermute | solution.py:22
  20.8 54.8 %collective-permute-start = (bf16[1,577,1024]{2,1,0:T(8,128)(2,1)S(1)}, bf16[1,577,1024]{2,1,0:T(8,128)(2,1)S(1)}, u32[]{:S(2)}, u32[]{:S(2)}) collective-permute-start(bf16[1,577,1024]{2,1,0:T(8,128)(2,1)S(1)} %get-tuple-element.404), channel_id=1, source_target_pairs={{0,1},{1,2},{2,3},{3,0},{4,5},{5,6},{6,7},{7,4},{8,9},{9,10},{10,1... | collective-permute-start | bytes 3545096 | tf_op jit(solution)/shard_map/ppermute | solution.py:22
  49.9 51.4 %collective-permute-start.4 = (bf16[1,577,1024]{2,1,0:T(8,128)(2,1)S(1)}, bf16[1,577,1024]{2,1,0:T(8,128)(2,1)}, u32[]{:S(2)}, u32[]{:S(2)}) collective-permute-start(bf16[1,577,1024]{2,1,0:T(8,128)(2,1)S(1)} %collective-permute-done.3), channel_id=1, source_target_pairs={{0,1},{1,2},{2,3},{3,0},{4,5},{5,6},{6,7},{7,4},{8,9},{9,10},{10,1... | collective-permute-start | bytes 3545096 | tf_op jit(solution)/shard_map/ppermute | solution.py:22
  75.6 51.4 %collective-permute-start.1 = (bf16[1,577,1024]{2,1,0:T(8,128)(2,1)S(1)}, bf16[1,577,1024]{2,1,0:T(8,128)(2,1)}, u32[]{:S(2)}, u32[]{:S(2)}) collective-permute-start(bf16[1,577,1024]{2,1,0:T(8,128)(2,1)S(1)} %collective-permute-done), channel_id=1, source_target_pairs={{0,1},{1,2},{2,3},{3,0},{4,5},{5,6},{6,7},{7,4},{8,9},{9,10},{10,1... | collective-permute-start | bytes 3545096 | tf_op jit(solution)/shard_map/ppermute | solution.py:22
  101.3 51.3 %collective-permute-start.5 = (bf16[1,577,1024]{2,1,0:T(8,128)(2,1)}, bf16[1,577,1024]{2,1,0:T(8,128)(2,1)}, u32[]{:S(2)}, u32[]{:S(2)}) collective-permute-start(bf16[1,577,1024]{2,1,0:T(8,128)(2,1)} %collective-permute-done.4), channel_id=1, source_target_pairs={{0,1},{1,2},{2,3},{3,0},{4,5},{5,6},{6,7},{7,4},{8,9},{9,10},{10,1... | collective-permute-start | bytes 3545096 | tf_op jit(solution)/shard_map/ppermute | solution.py:22
  102.4 304.0 %reduce-scatter.15.cloned.1.call-start = ((), (), s32[]{:S(2)}) async-start(), calls=%async_computation.15 | async-start | bytes 11960320 | tf_op jit(solution)/shard_map/reduce_scatter | solution.py:175
  126.9 50.4 %collective-permute-start.2 = (bf16[1,577,1024]{2,1,0:T(8,128)(2,1)}, bf16[1,577,1024]{2,1,0:T(8,128)(2,1)}, u32[]{:S(2)}, u32[]{:S(2)}) collective-permute-start(bf16[1,577,1024]{2,1,0:T(8,128)(2,1)} %collective-permute-done.1), channel_id=1, source_target_pairs={{0,1},{1,2},{2,3},{3,0},{4,5},{5,6},{6,7},{7,4},{8,9},{9,10},{10,1... | collective-permute-start | bytes 3545096 | tf_op jit(solution)/shard_map/ppermute | solution.py:22
  243.5 330.3 %reduce-scatter.11.cloned.1.call-start = ((), (), s32[]{:S(2)}) async-start(), calls=%async_computation.11 | async-start | bytes 11960320 | tf_op jit(solution)/shard_map/reduce_scatter | solution.py:175
  276.0 297.7 %copy-start.73 = (f32[1,1024]{1,0:T(1,128)S(1)}, f32[1,1024]{1,0:T(1,128)}, u32[]{:S(2)}) copy-start(f32[1,1024]{1,0:T(1,128)} %get-tuple-element.394) | copy-start | bytes 12292
  276.0 324.4 %all-gather.13.cloned.1.call-start = ((), (), s32[]{:S(2)}) async-start(), calls=%async_computation.13 | async-start | bytes 6291456 | tf_op jit(solution)/shard_map/all_gather | solution.py:134
  279.9 404.1 %all-gather.15.cloned.1.call-start = ((), (), s32[]{:S(2)}) async-start(), calls=%async_computation.16 | async-start | bytes 5980160 | tf_op jit(solution)/shard_map/all_gather | solution.py:183
  580.6 194.4 %all-gather.11.cloned.1.call-start = ((), (), s32[]{:S(2)}) async-start(), calls=%async_computation.12 | async-start | bytes 5980160 | tf_op jit(solution)/shard_map/all_gather | solution.py:183
  581.2 284.3 %all-gather.17.cloned.1.call-start = ((), (), s32[]{:S(2)}) async-start(), calls=%async_computation.18 | async-start | bytes 5980160 | tf_op jit(solution)/shard_map/all_gather | solution.py:197
  594.9 361.2 %all-gather.21.cloned.1.call-start = ((), (), s32[]{:S(2)}) async-start(), calls=%async_computation.22 | async-start | bytes 5980160 | tf_op jit(solution)/shard_map/all_gather | solution.py:197
  599.4 520.9 %reduce-scatter.19.cloned.1.call-start = ((), (), s32[]{:S(2)}) async-start(), calls=%async_computation.19 | async-start | bytes 11960320 | tf_op jit(solution)/shard_map/reduce_scatter | solution.py:209
  888.2 398.7 %reduce-scatter.23.cloned.1.call-start = ((), (), s32[]{:S(2)}) async-start(), calls=%async_computation.23 | async-start | bytes 11960320 | tf_op jit(solution)/shard_map/reduce_scatter | solution.py:209
  978.4 475.1 %reduce-scatter.13.cloned.1.call-start = ((), (), s32[]{:S(2)}) async-start(), calls=%async_computation.14 | async-start | bytes 11960320 | tf_op jit(solution)/shard_map/reduce_scatter | solution.py:189
  1035.0 585.6 %reduce-scatter.17.cloned.1.call-start = ((), (), s32[]{:S(2)}) async-start(), calls=%async_computation.17 | async-start | bytes 11960320 | tf_op jit(solution)/shard_map/reduce_scatter | solution.py:189
  1045.7 575.0 %copy-start.71 = (f32[1,1024]{1,0:T(1,128)S(1)}, f32[1,1024]{1,0:T(1,128)}, u32[]{:S(2)}) copy-start(f32[1,1024]{1,0:T(1,128)} %get-tuple-element.391) | copy-start | bytes 12292
  1045.7 677.9 %all-gather.19.cloned.1.call-start = ((), (), s32[]{:S(2)}) async-start(), calls=%async_computation.20 | async-start | bytes 5980160 | tf_op jit(solution)/shard_map/all_gather | solution.py:220
  1632.1 182.5 %all-gather.23.cloned.1.call-start = ((), (), s32[]{:S(2)}) async-start(), calls=%async_computation.24 | async-start | bytes 5980160 | tf_op jit(solution)/shard_map/all_gather | solution.py:220
  1636.6 289.5 %reduce-scatter.29.cloned.1.call-start = ((), (), s32[]{:S(2)}) async-start(), calls=%async_computation.27 | async-start | bytes 12582912 | tf_op jit(solution)/shard_map/reduce_scatter | solution.py:274
  1671.9 263.7 %reduce-scatter.27.cloned.1.call-start = ((), (), s32[]{:S(2)}) async-start(), calls=%async_computation.26 | async-start | bytes 6291456 | tf_op jit(solution)/shard_map/reduce_scatter | solution.py:273
  1911.8 167.9 %all-reduce.3.cloned.1.call-start = ((), (), s32[]{:S(2)}) async-start(), calls=%async_computation.28 | async-start | bytes 12582912 | tf_op jit(solution)/shard_map/psum | solution.py:292
  1942.7 302.6 %reduce-scatter.21.cloned.1.call-start = ((), (), s32[]{:S(2)}) async-start(), calls=%async_computation.21 | async-start | bytes 11960320 | tf_op jit(solution)/shard_map/reduce_scatter | solution.py:244
  1956.2 455.9 %reduce-scatter.25.cloned.1.call-start = ((), (), s32[]{:S(2)}) async-start(), calls=%async_computation.25 | async-start | bytes 11960320 | tf_op jit(solution)/shard_map/reduce_scatter | solution.py:244
  2120.1 292.0 %copy-start.2 = (bf16[1,1,1,577,1024]{4,3,2,1,0:T(8,128)(2,1)S(1)}, bf16[1,1,1,577,1024]{4,3,2,1,0:T(8,128)(2,1)}, u32[]{:S(2)}) copy-start(bf16[1,1,1,577,1024]{4,3,2,1,0:T(8,128)(2,1)} %copy-done.1) | copy-start | bytes 3545092
  2120.1 292.0 %copy-start.47 = (f32[577]{0:T(1024)S(1)}, f32[577]{0:T(1024)}, u32[]{:S(2)}) copy-start(f32[577]{0:T(1024)} %copy-done.46) | copy-start | bytes 6928
  2120.1 292.0 %copy-start.57 = (f32[577]{0:T(1024)S(1)}, f32[577]{0:T(1024)}, u32[]{:S(2)}) copy-start(f32[577]{0:T(1024)} %copy-done.56) | copy-start | bytes 6928
  2247.6 168.7 %copy-start.55 = (f32[577]{0:T(1024)S(1)}, f32[577]{0:T(1024)}, u32[]{:S(2)}) copy-start(f32[577]{0:T(1024)} %copy-done.54) | copy-start | bytes 6928
  2247.6 168.7 %copy-start.66 = (f32[577]{0:T(1024)S(1)}, f32[577]{0:T(1024)}, u32[]{:S(2)}) copy-start(f32[577]{0:T(1024)} %copy-done.65) | copy-start | bytes 6928
  (95 other events, 1580.9 us)
Sparse Core Ops, SparseCore 0:
  102.6 12.2 all-gather.8
  243.6 162.7 reduce-scatter.14
  409.5 164.2 reduce-scatter.10
  575.7 14.5 all-gather.12
  592.3 91.6 all-gather.14
  686.0 88.9 all-gather.10
  776.6 88.9 all-gather.16
  867.1 88.9 all-gather.20
  958.4 161.7 reduce-scatter.18
  1122.6 164.2 reduce-scatter.22
  1289.3 164.1 reduce-scatter.12
  1456.4 164.2 reduce-scatter.16
  1632.2 91.3 all-gather.18
  1725.6 88.9 all-gather.22
  1817.3 15.2 reduce-scatter.28
  1911.9 10.6 reduce-scatter.26
  1942.9 136.7 all-reduce.2
  2081.9 163.3 reduce-scatter.20
  2247.8 164.2 reduce-scatter.24
